TPU v7x, 256 devices: a whole 4x4x8 slice. The times are simulated.
256 devices in a mesh: tok: 32 (over z_lo, x, core), blk: 8 (over y, z_hi).
Axes of the slice: x: 4, y: 4, z: 8 (z_hi: 2, z_lo: 4; z = z_hi * 4 + z_lo), core: 2. Of those that a mesh axis runs over, the one named last changes fastest.
Arguments:
- activations: bfloat16 [4096, 7168], P('tok', 'blk'), may hold values from -600 to 600
- signs: float32 [7168], P('blk'), may hold values from -1 to 1, as said below
Outputs:
- hessian: float32 [7168, 7168], P('tok', 'blk')
- incoherence: float32 [7168], P('blk')
- largest_ratio: float32 [], replicated
Inputs may be any that keep to these rules, and one draw needn't show every extreme that they name: `signs`: every entry is -1 or 1.
All inputs are finite; a program needn't handle non-finite values.
Results may differ from a plain program's by a relative error of at most 0.0037.
Values may be sent and summed in bfloat16 or wider, within the bound.
A program may use at most 128 MiB of HBM per device.

v0:
```python
import math
import jax
import jax.numpy as jnp
import numpy as np
from jax import lax
from jax.sharding import PartitionSpec as P

WALSH = 512
MIX = 14
FEATURES = 7168
EPS = 1e-06
DAMP = 0.01


def walsh(length):
    table = np.ones((1, 1))
    while table.shape[0] < length:
        table = np.block([[table, table], [table, -table]])
    return table


def cosine(length):
    k = np.arange(length)[:, None]
    n = np.arange(length)[None, :]
    table = math.sqrt(2.0 / length) * np.cos(math.pi * (n + 0.5) * k / length)
    table[0] *= math.sqrt(0.5)
    return table


def split_table(local):
    table = np.kron(walsh(local), cosine(MIX).T) / math.sqrt(WALSH)
    high = table.astype(jnp.bfloat16)
    low = (table - high.astype(np.float64)).astype(jnp.bfloat16)
    return (high, low)


def contract_tokens(left, right):
    return lax.dot_general(
        left, right, (((0,), (0,)), ((), ())), preferred_element_type=jnp.float32
    )


def combine(parts):
    parts = list(parts)
    step = 1
    while step < len(parts):
        for i in range(0, len(parts), 2 * step):
            for j in range(i, i + step):
                parts[j], parts[j + step] = (parts[j] + parts[j + step], parts[j] - parts[j + step])
        step *= 2
    return parts


def per_device(activations, signs):
    rows, width = activations.shape
    blocks = lax.axis_size("blk")
    toks = lax.axis_size("tok")
    b = lax.axis_index("blk")
    t = lax.axis_index("tok")
    share = rows // blocks
    row_count = FEATURES // toks
    high, low = split_table(WALSH // blocks)
    signed = activations * signs.astype(jnp.bfloat16)[None, :]
    mine = lax.all_to_all(signed.reshape(blocks, share, width), "blk", 0, 0, tiled=True)
    flat = mine.reshape(blocks * share, width)
    mixed = jnp.dot(flat, high, preferred_element_type=jnp.float32)
    mixed = mixed + jnp.dot(flat, low, preferred_element_type=jnp.float32)
    mixed = mixed.reshape(blocks, share, width)
    rotated = jnp.stack(combine([mixed[i] for i in range(blocks)])).astype(jnp.bfloat16)
    wide = rotated.astype(jnp.float32)
    trace_total = lax.psum(jnp.sum(wide * wide), ("tok", "blk"))
    columns = lax.all_to_all(rotated, "blk", 0, 0, tiled=True).reshape(rows, width)
    columns = lax.all_gather(columns, "tok", axis=0, tiled=True)
    pieces = jnp.moveaxis(rotated, 0, 1).reshape(share, toks, row_count)
    pieces = lax.all_to_all(jnp.moveaxis(pieces, 1, 0), "tok", 0, 0, tiled=True)
    pieces = lax.all_gather(pieces, "blk", axis=1, tiled=False)
    left = pieces.reshape(toks * rows, row_count)
    gram = contract_tokens(left, columns)
    at_rows = t * row_count + jnp.arange(row_count, dtype=jnp.int32)[:, None]
    at_columns = b * width + jnp.arange(width, dtype=jnp.int32)[None, :]
    on_diag = at_rows == at_columns
    peaks = jnp.max(jnp.where(on_diag, 0.0, jnp.abs(gram)), axis=0)
    peak = lax.pmax(peaks, "tok")
    largest = lax.pmax(jnp.max(peak), "blk")
    diag_mean = trace_total / FEATURES + EPS
    hessian = gram / diag_mean + DAMP * on_diag.astype(jnp.float32)
    return (hessian, peak / diag_mean, largest / diag_mean)


def solution(mesh):
    return jax.shard_map(
        per_device,
        mesh=mesh,
        in_specs=(P("tok", "blk"), P("blk")),
        out_specs=(P("tok", "blk"), P("blk"), P()),
        check_vma=False,
    )
```

profile of v0, /device:TPU:0, one launch (start us, length us, event | category | flops | bytes accessed | tf_op | source)
XLA Modules:
  0.0 306.4 jit_solution(10132613297484152521)
XLA Ops:
  7.2 0.0 copy-start
  7.2 0.0 all-gather.6.cloned.1.call-start
  7.2 0.8 convert_element_type.8
  8.0 1.0 broadcast_multiply_fusion
  9.0 20.2 %all_to_all.15 = bf16[8,16,896]{2,1,0:T(8,128)(2,1)S(1)} all-to-all(bf16[8,16,896]{2,1,0:T(8,128)(2,1)S(1)} %bitcast.56), channel_id=1, replica_groups=mesh['tok'=32,'blk'=8] {'blk'}, dimensions={0} | all-to-all | bytes 458752 | tf_op jit(solution)/shard_map/all_to_all | solution.py:64
  29.2 1.9 fusion.22
  31.1 0.0 copy-done
  31.1 0.4 convolution_add_fusion
  31.8 0.2 reshape.51
  32.0 0.2 copy.10
  32.2 18.7 %all_to_all.16 = bf16[32,16,224]{2,1,0:T(8,128)(2,1)S(1)} all-to-all(bf16[32,16,224]{2,1,0:T(8,128)(2,1)S(1)} %copy.10), channel_id=1, replica_groups=mesh['tok'=32,'blk'=8] {'tok'}, dimensions={0} | all-to-all | bytes 458752 | tf_op jit(solution)/shard_map/all_to_all | solution.py:75
  50.9 0.8 copy.11
  51.7 0.0 all-gather.6.cloned.1.call-update
  51.8 0.0 all-gather.4.cloned.1.call-start
  51.8 14.7 %all_to_all.17 = bf16[8,16,896]{2,1,0:T(8,128)(2,1)} all-to-all(bf16[8,16,896]{2,1,0:T(8,128)(2,1)S(1)} %fusion.20), channel_id=1, replica_groups=mesh['tok'=32,'blk'=8] {'blk'}, dimensions={0} | all-to-all | bytes 458752 | tf_op jit(solution)/shard_map/all_to_all | solution.py:72
  66.5 0.0 all-gather.4.cloned.1.call-update
  66.6 0.7 multiply_reduce_fusion
  67.3 90.8 %psum.7 = f32[]{:T(128)} all-reduce(f32[]{:T(128)} %multiply_reduce_fusion), channel_id=1, replica_groups=mesh['tok'=32,'blk'=8] {'tok','blk'}, use_global_device_ids=true, to_apply=%region_1.0 | all-reduce | flops 1 | bytes 8 | tf_op jit(solution)/shard_map/psum | solution.py:71
  158.7 0.0 all-gather.6.cloned.1.call-done
  158.7 4.1 %copy.12 = bf16[32,128,224]{1,0,2:T(8,128)(2,1)S(1)} copy(bf16[32,128,224]{2,0,1:T(8,128)(2,1)} %all-gather.6.cloned.1.call-done) | data formatting | bytes 3670016 | tf_op jit(solution)/shard_map/all_gather | solution.py:76
  162.8 26.1 %all-gather.4.cloned.1.call-done = bf16[4096,896]{1,0:T(8,128)(2,1)} async-done(((bf16[128,896]{1,0:T(8,128)(2,1)}), bf16[4096,896]{1,0:T(8,128)(2,1)}) %all-gather.4.cloned.1.call-update) | async-done | bytes 7340048 | tf_op jit(solution)/shard_map/all_gather | solution.py:73
  188.9 6.5 %fusion.4 = (f32[896]{0:T(1024)S(1)}, f32[224,896]{1,0:T(8,128)}) fusion(s32[896]{0:T(1024)S(1)} %iota_add_fusion, s32[224]{0:T(256)S(1)} %iota_add_fusion.1, f32[]{:T(128)S(6)} %add.82, bf16[4096,896]{1,0:T(8,128)(2,1)} %all-gather.4.cloned.1.call-done, bf16[28,8,32,128]{3,2,1,0:T(8,128)(2,1)S(1)} %bitcast.53), kind=kOutput, calls=%fused_computation.7 | convolution fusion | flops 1645571200 | bytes 9985924 | tf_op jit(solution)/shard_map/dot_general | solution.py:38
  195.4 69.8 %pmax.14 = f32[896]{0:T(1024)S(1)} all-reduce(f32[896]{0:T(1024)S(1)} %get-tuple-element.13), channel_id=1, replica_groups=mesh['tok'=32,'blk'=8] {'tok'}, use_global_device_ids=true, to_apply=%region_3.4 | all-reduce | flops 896 | bytes 7168 | tf_op jit(solution)/shard_map/pmax | solution.py:83
  265.3 1.2 fusion.21
  266.5 31.3 %pmax.15 = f32[]{:T(128)} all-reduce(f32[]{:T(128)} %get-tuple-element.15), channel_id=1, replica_groups=mesh['tok'=32,'blk'=8] {'blk'}, use_global_device_ids=true, to_apply=%region_5.6 | all-reduce | flops 1 | bytes 8 | tf_op jit(solution)/shard_map/pmax | solution.py:84
  (11 shorter events, 0.3 us)
Async XLA Ops:
  7.2 23.9 %copy-start = (bf16[896,896]{1,0:T(8,128)(2,1)S(1)}, bf16[896,896]{1,0:T(8,128)(2,1)}, u32[]{:S(2)}) copy-start(bf16[896,896]{1,0:T(8,128)(2,1)} %constant.30.clone) | copy-start | bytes 4816900
  7.2 151.6 %all-gather.6.cloned.1.call-start = ((), (), s32[]{:S(2)}) async-start(), calls=%async_computation.4 | async-start | bytes 2359296 | tf_op jit(solution)/shard_map/all_gather | solution.py:76
  51.8 137.2 %all-gather.4.cloned.1.call-start = ((), (), s32[]{:S(2)}) async-start(), calls=%async_computation.3 | async-start | bytes 7569408 | tf_op jit(solution)/shard_map/all_gather | solution.py:73
Sparse Core Ops, SparseCore 0:
  51.9 71.4 all-gather.5
  125.2 63.6 all-gather.3
where the time goes:
time: 307 us; the launch traced here: 306 us
  blocking collectives  246 us (80%)
  waiting for transfers between devices  26.1 us (9%)
  between operations  16.6 us (5%)
  matrix products  8.8 us (3%)
  local copies, waits for them, and re-layouts  5.31 us (2%)
  other arithmetic  3.89 us (1%)
    psum x1, blocking collectives, per_device(): trace_total = lax.psum(jnp.sum(wide * wide), ('tok', 'blk'))  90.8 us
    pmax x1, blocking collectives, per_device(): peak = lax.pmax(peaks, 'tok')  69.8 us
    pmax x1, blocking collectives, per_device(): largest = lax.pmax(jnp.max(peak), 'blk')  31.3 us
    all_gather x1, waiting for transfers between devices, per_device(): columns = lax.all_gather(columns, 'tok', axis=0, tiled=True)  26.1 us
    all_to_all x1, blocking collectives, per_device(): lax.all_to_all(signed.reshape(blocks, share, width), 'blk', 0, 0, tiled=T...  20.2 us
    all_to_all x1, blocking collectives, per_device(): pieces = lax.all_to_all(jnp.moveaxis(pieces, 1, 0), 'tok', 0, 0, tiled=True)  18.7 us
    all_to_all x1, blocking collectives, per_device(): lax.all_to_all(rotated, 'blk', 0, 0, tiled=True).reshape(rows, width)  14.7 us
    dot_general x1, matrix products, contract_tokens(): lax.dot_general(left, right, (((0,), (0,)), ((), ())), preferred_element_...  6.5 us
  transfers between devices with their start and end apart: 2, of which 1 were waited for; matrix products, arithmetic and copies ran while one was open for 2% of the time, Pallas kernels for 0%

commit v1 on v0

--- a/solution.py
+++ b/solution.py
@@ -70,7 +70,9 @@
     wide = rotated.astype(jnp.float32)
     trace_total = lax.psum(jnp.sum(wide * wide), ("tok", "blk"))
     columns = lax.all_to_all(rotated, "blk", 0, 0, tiled=True).reshape(rows, width)
-    columns = lax.all_gather(columns, "tok", axis=0, tiled=True)
+    columns = jnp.concatenate(
+        lax.all_to_all(jnp.stack([columns] * lax.axis_size("tok")), "tok", 0, 0), axis=0
+    )
     pieces = jnp.moveaxis(rotated, 0, 1).reshape(share, toks, row_count)
     pieces = lax.all_to_all(jnp.moveaxis(pieces, 1, 0), "tok", 0, 0, tiled=True)
     pieces = lax.all_gather(pieces, "blk", axis=1, tiled=False)

time: 307 us -> 431 us (1.40)
  blocking collectives: 246 us -> 367 us
  waiting for transfers between devices: 26.1 us -> 9.66 us
  starting transfers between devices: 0.08 us -> 8.35 us
  other arithmetic: 3.89 us -> 9.64 us
  local copies, waits for them, and re-layouts: 5.31 us -> 10.3 us
    psum x1, blocking collectives: 90.8 us -> 229 us  [per_device(): trace_total = lax.psum(jnp.sum(wide * wide), ('tok', 'blk'))]
    all_gather x1 -> x0, waiting for transfers between devices: 26.1 us -> none  [per_device(): columns = lax.all_gather(columns, 'tok', axis=0, tiled=True)]
    all_to_all x1 -> x0, blocking collectives: 14.7 us -> none  [per_device(): lax.all_to_all(rotated, 'blk', 0, 0, tiled=True).reshape(rows, width)]
    all_to_all x0 -> x2, waiting for transfers between devices: none -> 9.63 us  [the longest x1 9.62 us: per_device(): lax.all_to_all(rotated, 'blk', 0, 0, tiled=True).reshape(rows, width)]
    all_to_all x0 -> x2, starting transfers between devices: none -> 8.31 us  [the longest x1 4.91 us: per_device(): lax.all_to_all(jnp.stack([columns] * lax.axis_size('tok')), 'tok', 0, 0)]
  transfers between devices with their start and end apart: 2 -> 3, of which waited for: 1 -> 1; matrix products, arithmetic and copies ran while one was open for 2% -> 2% of each run, Pallas kernels for 0% -> 0%
where the time goes in v1:
time: 431 us; the launch traced here: 430 us
  blocking collectives  367 us (85%)
  between operations  16.6 us (4%)
  local copies, waits for them, and re-layouts  10.3 us (2%)
  waiting for transfers between devices  9.66 us (2%)
  other arithmetic  9.64 us (2%)
  matrix products  8.58 us (2%)
  starting transfers between devices  8.35 us (2%)
    psum x1, blocking collectives, per_device(): trace_total = lax.psum(jnp.sum(wide * wide), ('tok', 'blk'))  229 us
    pmax x1, blocking collectives, per_device(): peak = lax.pmax(peaks, 'tok')  70.2 us
    pmax x1, blocking collectives, per_device(): largest = lax.pmax(jnp.max(peak), 'blk')  28 us
    all_to_all x1, blocking collectives, per_device(): lax.all_to_all(signed.reshape(blocks, share, width), 'blk', 0, 0, tiled=T...  20.2 us
    all_to_all x1, blocking collectives, per_device(): pieces = lax.all_to_all(jnp.moveaxis(pieces, 1, 0), 'tok', 0, 0, tiled=True)  19 us
    all_to_all x1, waiting for transfers between devices, per_device(): lax.all_to_all(rotated, 'blk', 0, 0, tiled=True).reshape(rows, width)  9.62 us
  transfers between devices with their start and end apart: 3, of which 1 were waited for; matrix products, arithmetic and copies ran while one was open for 2% of the time, Pallas kernels for 0%

profile of v1, /device:TPU:0, one launch (start us, length us, event | category | flops | bytes accessed | tf_op | source)
XLA Modules:
  0.0 430.0 jit_solution(6528080680008196636)
XLA Ops:
  7.2 0.0 copy-start
  7.2 0.8 convert_element_type.8
  8.0 1.0 broadcast_multiply_fusion
  9.0 20.2 %all_to_all.20 = bf16[8,16,896]{2,1,0:T(8,128)(2,1)S(1)} all-to-all(bf16[8,16,896]{2,1,0:T(8,128)(2,1)S(1)} %bitcast.55), channel_id=1, replica_groups=mesh['tok'=32,'blk'=8] {'blk'}, dimensions={0} | all-to-all | bytes 458752 | tf_op jit(solution)/shard_map/all_to_all | solution.py:64
  29.2 1.9 fusion.22
  31.0 0.0 copy-done
  31.0 0.4 convolution_add_fusion
  31.5 0.6 fusion.6
  32.1 0.6 fusion.8
  32.7 0.6 fusion.10
  33.4 0.6 fusion.12
  34.0 0.6 fusion.14
  34.6 0.6 fusion.16
  35.2 0.6 fusion.18
  35.9 0.6 fusion.20
  36.5 3.4 all-to-all-start.2
  39.9 1.0 copy.9
  40.9 0.2 reshape.53
  41.2 0.2 copy.10
  41.3 9.6 %all-to-all-done.2 = bf16[8,16,896]{2,1,0:T(8,128)(2,1)S(1)} async-done(((bf16[8,16,896]{2,1,0:T(8,128)(2,1)}), bf16[8,16,896]{2,1,0:T(8,128)(2,1)S(1)}, u32[]{:S(2)}, u32[]{:S(2)}) %all-to-all-start.2) | async-done | bytes 229408 | tf_op jit(solution)/shard_map/all_to_all | solution.py:72
  50.9 19.0 %all_to_all.21 = bf16[32,16,224]{2,1,0:T(8,128)(2,1)S(1)} all-to-all(bf16[32,16,224]{2,1,0:T(8,128)(2,1)S(1)} %copy.10), channel_id=1, replica_groups=mesh['tok'=32,'blk'=8] {'tok'}, dimensions={0} | all-to-all | bytes 458752 | tf_op jit(solution)/shard_map/all_to_all | solution.py:77
  69.9 4.1 stack.48
  74.0 4.9 %all-to-all-start.3 = ((bf16[32,128,896]{2,1,0:T(8,128)(2,1)}), bf16[32,128,896]{2,1,0:T(8,128)(2,1)}, u32[]{:S(2)}, u32[]{:S(2)}) async-start(bf16[32,128,896]{2,1,0:T(8,128)(2,1)} %stack.48), calls=%async_computation.3 | async-start | bytes 14680064 | tf_op jit(solution)/shard_map/all_to_all | solution.py:74
  78.9 0.0 all-gather.3.cloned.1.call-start
  78.9 0.8 copy.11
  79.7 0.0 all-gather.3.cloned.1.call-update
  79.8 1.7 multiply_reduce_fusion
  81.4 229.4 %psum.7 = f32[]{:T(128)} all-reduce(f32[]{:T(128)} %multiply_reduce_fusion), channel_id=1, replica_groups=mesh['tok'=32,'blk'=8] {'tok','blk'}, use_global_device_ids=true, to_apply=%region_1.0 | all-reduce | flops 1 | bytes 8 | tf_op jit(solution)/shard_map/psum | solution.py:71
  311.5 0.0 all-gather.3.cloned.1.call-done
  311.5 4.1 copy.12
  315.6 0.0 all-to-all-done.3
  315.6 6.3 %fusion.4 = (f32[896]{0:T(1024)S(1)}, f32[224,896]{1,0:T(8,128)}) fusion(s32[896]{0:T(1024)S(1)} %iota_add_fusion, s32[224]{0:T(256)S(1)} %iota_add_fusion.1, f32[]{:T(128)S(6)} %add.82, bf16[4096,896]{1,0:T(8,128)(2,1)} %bitcast.13, bf16[28,8,32,128]{3,2,1,0:T(8,128)(2,1)S(1)} %bitcast.53), kind=kOutput, calls=%fused_computation.7 | convolution fusion | flops 1645571200 | bytes 9985924 | tf_op jit(solution)/shard_map/dot_general | solution.py:38
  321.9 70.2 %pmax.14 = f32[896]{0:T(1024)S(1)} all-reduce(f32[896]{0:T(1024)S(1)} %get-tuple-element.13), channel_id=1, replica_groups=mesh['tok'=32,'blk'=8] {'tok'}, use_global_device_ids=true, to_apply=%region_3.4 | all-reduce | flops 896 | bytes 7168 | tf_op jit(solution)/shard_map/pmax | solution.py:85
  392.1 1.2 fusion.21
  393.3 28.0 %pmax.15 = f32[]{:T(128)} all-reduce(f32[]{:T(128)} %get-tuple-element.15), channel_id=1, replica_groups=mesh['tok'=32,'blk'=8] {'blk'}, use_global_device_ids=true, to_apply=%region_5.6 | all-reduce | flops 1 | bytes 8 | tf_op jit(solution)/shard_map/pmax | solution.py:86
  (2 shorter events, 0.0 us)
Async XLA Ops:
  7.2 23.9 %copy-start = (bf16[896,896]{1,0:T(8,128)(2,1)S(1)}, bf16[896,896]{1,0:T(8,128)(2,1)}, u32[]{:S(2)}) copy-start(bf16[896,896]{1,0:T(8,128)(2,1)} %constant.30.clone) | copy-start | bytes 4816900
  36.5 14.5 %all-to-all-start.2 = ((bf16[8,16,896]{2,1,0:T(8,128)(2,1)}), bf16[8,16,896]{2,1,0:T(8,128)(2,1)S(1)}, u32[]{:S(2)}, u32[]{:S(2)}) async-start(bf16[8,16,896]{2,1,0:T(8,128)(2,1)} %fusion.20), calls=%async_computation.2 | async-start | bytes 458752 | tf_op jit(solution)/shard_map/all_to_all | solution.py:72
  74.0 241.6 %all-to-all-start.3 = ((bf16[32,128,896]{2,1,0:T(8,128)(2,1)}), bf16[32,128,896]{2,1,0:T(8,128)(2,1)}, u32[]{:S(2)}, u32[]{:S(2)}) async-start(bf16[32,128,896]{2,1,0:T(8,128)(2,1)} %stack.48), calls=%async_computation.3 | async-start | bytes 14680064 | tf_op jit(solution)/shard_map/all_to_all | solution.py:74
  78.9 232.6 %all-gather.3.cloned.1.call-start = ((), (), s32[]{:S(2)}) async-start(), calls=%async_computation.4 | async-start | bytes 2359296 | tf_op jit(solution)/shard_map/all_gather | solution.py:78
Sparse Core Ops, SparseCore 0:
  82.9 88.9 all-gather.2
